TPU v7x, 32 devices: a whole 2x2x4 slice. The times are simulated.
32 devices in a mesh: gx: 4 (over y, x), gy: 2 (over core), gz: 4 (over z).
Axes of the slice: x: 2, y: 2, z: 4, core: 2. Of those that a mesh axis runs over, the one named last changes fastest.
Arguments:
- spectrum: float32 [3, 2, 16, 16, 2048], P(None, None, ('gy', 'gx'), None, 'gz'), may hold values from -0.3125 to 0.3125
- theta: float32 [16, 16, 8192], P('gy', 'gz', 'gx'), may hold values from -6 to 6
- section_sum: float32 [16, 16, 8192], P('gy', 'gz', 'gx'), may hold values from -6 to 6
- seg_offset: int32 [4], replicated, may hold values from 0 to 2560, as said below
- seg_length: int32 [4], replicated, may hold values from 512 to 1536, as said below
- stencil_index: int32 [8, 8192], replicated, may hold values from 0 to 1535, as said below
- stencil_weight: float32 [8, 8192], replicated, may hold values from 0 to 0.25
Outputs:
- theta_next: float32 [16, 16, 8192], P('gy', 'gz', 'gx')
- section_next: float32 [16, 16, 8192], P('gy', 'gz', 'gx')
Inputs may be any that keep to these rules, and one draw needn't show every extreme that they name: `seg_length`: some block's segment holds exactly 1536 cells. For every block i, seg_offset[i] + 1536 <= 4096. `stencil_index`: positions count from the start of the segment of the scalar cell's x block; taps at or past that segment's length are padding.
All inputs are finite; a program needn't handle non-finite values.
Results may differ from a plain program's by a relative error of at most 0.00005.
Values sent between devices are 32-bit elements; how exact they have to be, the bound alone decides.
A program may use at most 64 MiB of HBM per device.

v0:
```python
import functools
import math

import jax
import jax.numpy as jnp
import numpy as np
from jax import lax
from jax.experimental import pallas as pl
from jax.experimental.pallas import tpu as pltpu
from jax.sharding import PartitionSpec as P

MESH = pl.DeviceIdType.MESH
VMEM = pltpu.VMEM
LANES = 128
HALO = 4

first_coeffs = (0.8, -0.2, 4.0 / 105.0, -1.0 / 280.0)
second_coeffs = (1.6, -0.2, 8.0 / 315.0, -1.0 / 560.0)
center_coeff = -205.0 / 72.0
diffusivity = 0.15
time_step = 0.4
section_keep = -5.0 / 9.0
section_gain = 15.0 / 16.0


def whole_vmem(count):
    return [pl.BlockSpec(memory_space=VMEM)] * count


def rotate(value, turn):
    re, im = value
    cosine, sine = math.cos(2 * math.pi * turn), math.sin(2 * math.pi * turn)
    quarter = turn * 4 % 4
    if quarter == 0:
        return re, im
    if quarter == 1:
        return -im, re
    if quarter == 2:
        return -re, -im
    if quarter == 3:
        return im, -re
    return re * cosine - im * sine, re * sine + im * cosine


def fft(values):
    count = len(values)
    if count == 1:
        return values
    even = fft(values[0::2])
    odd = fft(values[1::2])
    low, high = [], []
    for x in range(count // 2):
        re, im = rotate(odd[x], x / count)
        low.append((even[x][0] + re, even[x][1] + im))
        high.append((even[x][0] - re, even[x][1] - im))
    return low + high


def split(value):
    top = value.astype(jnp.bfloat16)
    return top, (value - top.astype(jnp.float32)).astype(jnp.bfloat16)


def section_kernel(
    sizes, span,
    offset_ref, length_ref, spec_ref, theta_ref, sum_ref, index_ref, weight_ref, twist_ref, last_ref,
    theta_out, sum_out,
    modes_send, modes_recv, mixed, velocity, seg_send, seg_recv, matrix_top, matrix_rest, gathered, values,
    grads, laplace, deep, x_back, x_front, y_back, y_front, z_back, z_front,
    modes_sems, seg_sems, face_sems,
):
    gx, gy, gz = sizes
    here = {axis: lax.axis_index(axis) for axis in ("gx", "gy", "gz")}
    counts = dict(gx=gx, gy=gy, gz=gz)
    ahead = {axis: {axis: lax.rem(here[axis] + 1, counts[axis])} for axis in here}
    behind = {axis: {axis: lax.rem(here[axis] + counts[axis] - 1, counts[axis])} for axis in here}
    rows, depth, cells = theta_ref.shape
    _, _, own_rows, all_depth, modes = spec_ref.shape
    local_slabs = modes // LANES
    group = own_rows * depth
    slabs = gz * local_slabs
    near = 2 * slabs
    far = 2 * slabs
    taps = index_ref.shape[0]

    barrier = pltpu.get_barrier_semaphore()
    targets = [{"gx": lax.rem(here["gx"] + step, gx)} for step in range(1, gx)]
    targets += [{"gz": lax.rem(here["gz"] + step, gz)} for step in range(1, gz)]
    targets += [ahead["gy"], behind["gy"]]
    for target in targets:
        pl.semaphore_signal(barrier, inc=1, device_id=target, device_id_type=MESH)

    for comp in range(3):
        for slab in range(local_slabs):
            for part in range(2):
                for row in range(own_rows):
                    held = spec_ref[comp, part, row, :, slab * LANES : (slab + 1) * LANES]
                    at = part * group + row * depth
                    for peer in range(gz):
                        modes_send[comp, peer, slab, at : at + depth, :] = held[
                            peer * depth : (peer + 1) * depth
                        ]
    pl.semaphore_wait(barrier, len(targets))

    def modes_copy(comp, step):
        target = lax.rem(here["gz"] + step, gz)
        return pltpu.make_async_remote_copy(
            src_ref=modes_send.at[comp, target],
            dst_ref=modes_recv.at[comp, here["gz"]],
            send_sem=modes_sems.at[0, comp, step - 1],
            recv_sem=modes_sems.at[1, comp, step - 1],
            device_id={"gz": target},
            device_id_type=MESH,
        )

    def seg_copy(comp, step):
        target = lax.rem(here["gx"] + step, gx)
        return pltpu.make_async_remote_copy(
            src_ref=seg_send.at[comp, target],
            dst_ref=seg_recv.at[comp, here["gx"]],
            send_sem=seg_sems.at[0, comp, step - 1],
            recv_sem=seg_sems.at[1, comp, step - 1],
            device_id={"gx": target},
            device_id_type=MESH,
        )

    faces = [
        pltpu.make_async_remote_copy(
            src_ref=source,
            dst_ref=place,
            send_sem=face_sems.at[0, number],
            recv_sem=face_sems.at[1, number],
            device_id=device,
            device_id_type=MESH,
        )
        for number, (source, place, device) in enumerate(
            [
                (theta_ref.at[:, :, pl.ds(cells - LANES, LANES)], x_back, ahead["gx"]),
                (theta_ref.at[:, :, pl.ds(0, LANES)], x_front, behind["gx"]),
                (theta_ref.at[pl.ds(rows - HALO, HALO)], y_back, ahead["gy"]),
                (theta_ref.at[pl.ds(0, HALO)], y_front, behind["gy"]),
                (theta_ref.at[:, pl.ds(depth - HALO, HALO), :], z_back, ahead["gz"]),
                (theta_ref.at[:, pl.ds(0, HALO), :], z_front, behind["gz"]),
            ]
        )
    ]
    for comp in range(3):
        for step in range(1, gz):
            modes_copy(comp, step).start()
    for face in faces:
        face.start()
    for comp in range(3):
        modes_recv[comp, here["gz"]] = modes_send[comp, here["gz"]]

    me = here["gx"]
    live_count = length_ref[me]
    begin = offset_ref[me] - jnp.minimum(offset_ref[me] // LANES, far - span) * LANES
    counter = lax.broadcasted_iota(jnp.int32, (LANES, LANES), 0).astype(jnp.float32).astype(jnp.bfloat16)

    def spread(row):
        one = jnp.broadcast_to(row, (16, LANES)).astype(jnp.bfloat16)
        return jnp.concatenate([one] * (LANES // 16), axis=0)

    def build(chunk, carry):
        columns = pl.ds(pl.multiple_of(me * cells + chunk * LANES, LANES), LANES)
        index = index_ref[:, columns]
        live = index < live_count
        weight = jnp.where(live, weight_ref[:, columns], 0.0)
        merged = jnp.zeros_like(weight)
        for tap in range(taps):
            merged = merged + jnp.where(index == index[tap : tap + 1], weight[tap : tap + 1], 0.0)
        high, low = split(merged)
        high, low = high.astype(jnp.float32), low.astype(jnp.float32)
        place = jnp.where(live, index + begin, -1)
        tops = [spread(high[tap : tap + 1]) for tap in range(taps)]
        rests = [spread(low[tap : tap + 1]) for tap in range(taps)]

        def slab_of(slab, inner):
            close = jnp.clip(place - slab * LANES, -1, LANES).astype(jnp.float32)
            top = jnp.zeros((LANES, LANES), jnp.bfloat16)
            rest = jnp.zeros((LANES, LANES), jnp.bfloat16)
            for tap in range(taps):
                hit = counter == spread(close[tap : tap + 1])
                top = jnp.where(hit, tops[tap], top)
                rest = jnp.where(hit, rests[tap], rest)
            at = pl.ds(pl.multiple_of(slab * LANES, LANES), LANES)
            matrix_top[chunk, at, :] = top
            matrix_rest[chunk, at, :] = rest
            return inner

        return lax.fori_loop(0, span, slab_of, carry)

    lax.fori_loop(0, cells // LANES, build, 0)

    last_both = last_ref[...]
    last_top = last_both[:far]
    dims = (((1,), (1,)), ((), ()))

    def twisted(line):
        re, im = mixed[:, line, :], mixed[:, group + line, :]
        pieces = []
        for quarter in range(LANES // near):
            part = slice(quarter * near, (quarter + 1) * near)
            cosine, sine = twist_ref[0, part, :], twist_ref[1, part, :]
            pieces.append(jnp.concatenate([re * cosine - im * sine, re * sine + im * cosine], axis=1))
        return jnp.concatenate(pieces, axis=0)

    def transform(comp, carry):
        for step in range(1, gz):
            modes_copy(comp, step).wait()

        def arrived(k):
            held = modes_recv[comp, k // local_slabs, k % local_slabs]
            return held[:group], held[group:]

        for parity in range(2):
            mixes = fft([rotate(arrived(k), parity * k / near) for k in range(slabs)])
            for x in range(slabs):
                mixed[2 * x + parity, 0:group, :] = mixes[x][0]
                mixed[2 * x + parity, group:, :] = mixes[x][1]
        for pair in range(group // 2):
            turned = jnp.concatenate([twisted(2 * pair), twisted(2 * pair + 1)], axis=0)
            top, rest = split(turned)
            first = lax.dot_general(last_both, top, dims, preferred_element_type=jnp.float32)
            second = lax.dot_general(last_top, rest, dims, preferred_element_type=jnp.float32)
            total = first[:far] + (first[far:] + second)
            velocity[:, 2 * pair, :] = total[:, :LANES]
            velocity[:, 2 * pair + 1, :] = total[:, LANES:]
        for block in range(gx):
            start = jnp.minimum(offset_ref[block] // LANES, far - span)
            seg_send[comp, block] = velocity[pl.ds(start, span)]
        for step in range(1, gx):
            seg_copy(comp, step).start()
        seg_recv[comp, me] = seg_send[comp, me]
        return carry

    lax.fori_loop(0, 3, transform, 0)

    for face in faces[:4]:
        face.wait()

    def line(row):
        if row < 0:
            return y_back[HALO + row]
        if row >= rows:
            return y_front[row - rows]
        return theta_ref[row]

    for row in range(rows):
        at = slice(row * depth, (row + 1) * depth)
        center = theta_ref[row]
        wide = jnp.concatenate([x_back[row], center, x_front[row]], axis=1)
        width = wide.shape[1]
        grad_x = jnp.zeros_like(center)
        grad_y = jnp.zeros_like(center)
        partial = 3.0 * center_coeff * center
        for reach in range(1, 5):
            ahead_x = pltpu.roll(wide, width - reach, 1)[:, LANES : LANES + cells]
            behind_x = pltpu.roll(wide, reach, 1)[:, LANES : LANES + cells]
            ahead_y, behind_y = line(row + reach), line(row - reach)
            grad_x = grad_x + first_coeffs[reach - 1] * (ahead_x - behind_x)
            grad_y = grad_y + first_coeffs[reach - 1] * (ahead_y - behind_y)
            partial = partial + second_coeffs[reach - 1] * (ahead_x + behind_x + ahead_y + behind_y)
        grads[0, at, :] = grad_x
        grads[1, at, :] = grad_y
        laplace[at, :] = partial
    for face in faces[4:]:
        face.wait()
    deep[:, 0:HALO, :] = z_back[...]
    deep[:, HALO : HALO + depth, :] = theta_ref[...]
    deep[:, HALO + depth :, :] = z_front[...]
    for row in range(rows):
        at = slice(row * depth, (row + 1) * depth)
        grad_z = jnp.zeros((depth, cells), jnp.float32)
        partial = laplace[at, :]
        for reach in range(1, 5):
            ahead_z = deep[row, HALO + reach : HALO + reach + depth]
            behind_z = deep[row, HALO - reach : HALO - reach + depth]
            grad_z = grad_z + first_coeffs[reach - 1] * (ahead_z - behind_z)
            partial = partial + second_coeffs[reach - 1] * (ahead_z + behind_z)
        grads[2, at, :] = grad_z
        change = diffusivity * partial
        laplace[at, :] = section_keep * sum_ref[row] + time_step * change

    for comp in range(3):
        for step in range(1, gx):
            seg_copy(comp, step).wait()
    lines = gx * group
    for comp in range(3):
        for block in range(gx):
            at = (comp * gx + block) * group
            for slab in range(span):
                gathered[at : at + group, slab * LANES : (slab + 1) * LANES] = seg_recv[comp, block, slab]
    total = 3 * lines
    top, rest = split(gathered[...])
    values[0:total, :] = top
    values[total:, :] = rest

    def combine(pair, carry):
        top = jnp.concatenate([matrix_top[2 * pair], matrix_top[2 * pair + 1]], axis=1)
        rest = jnp.concatenate([matrix_rest[2 * pair], matrix_rest[2 * pair + 1]], axis=1)
        first = jnp.dot(values[...], top, preferred_element_type=jnp.float32)
        second = jnp.dot(values[0:total, :], rest, preferred_element_type=jnp.float32)
        moved = first[:total] + (first[total:] + second)
        columns = pl.ds(pl.multiple_of(pair * 2 * LANES, 2 * LANES), 2 * LANES)
        carried = None
        for comp in range(3):
            term = moved[comp * lines : (comp + 1) * lines] * grads[comp, :, columns]
            carried = term if carried is None else carried + term
        after = laplace[:, columns] - time_step * carried
        for row in range(rows):
            piece = after[row * depth : (row + 1) * depth]
            sum_out[row, :, columns] = piece
            theta_out[row, :, columns] = theta_ref[row, :, columns] + section_gain * piece
        return carry

    lax.fori_loop(0, cells // (2 * LANES), combine, 0)


def body(spectrum, theta, section_sum, seg_offset, seg_length, stencil_index, stencil_weight):
    sizes = tuple(lax.axis_size(axis) for axis in ("gx", "gy", "gz"))
    gx, _, gz = sizes
    _, _, own_rows, all_depth, modes = spectrum.shape
    rows, depth, cells = theta.shape
    group = own_rows * depth
    slabs = gz * modes // LANES
    length = 2 * slabs * LANES
    far = length // LANES
    span = min(3 * length // (2 * gx) // LANES + 1, far)
    k = np.arange(LANES)
    turn = 2 * np.pi * (np.outer(k, k) % length) / length
    twist = np.stack([np.cos(turn), np.sin(turn)]).astype(np.float32)
    turn = 2 * np.pi * (np.outer(np.arange(far), k) % far) / far
    last = np.concatenate([np.cos(turn), -np.sin(turn)], axis=1).astype(np.float32)
    top = last.astype(jnp.bfloat16)
    rest = (last - top.astype(np.float32)).astype(jnp.bfloat16)
    modes_shape = (3, gz, modes // LANES, 2 * group, LANES)
    seg_shape = (3, gx, span, group, LANES)
    lines = gx * group
    single = jnp.float32
    return tuple(
        pl.pallas_call(
            functools.partial(section_kernel, sizes, span),
            out_shape=[jax.ShapeDtypeStruct(theta.shape, single)] * 2,
            in_specs=[pl.BlockSpec(memory_space=pltpu.SMEM)] * 2 + whole_vmem(7),
            out_specs=whole_vmem(2),
            scratch_shapes=[
                VMEM(modes_shape, single),
                VMEM(modes_shape, single),
                VMEM((2 * slabs, 2 * group, LANES), single),
                VMEM((far, group, LANES), single),
                VMEM(seg_shape, single),
                VMEM(seg_shape, single),
                VMEM((cells // LANES, span * LANES, LANES), jnp.bfloat16),
                VMEM((cells // LANES, span * LANES, LANES), jnp.bfloat16),
                VMEM((3 * lines, span * LANES), single),
                VMEM((6 * lines, span * LANES), jnp.bfloat16),
                VMEM((3, rows * depth, cells), single),
                VMEM((rows * depth, cells), single),
                VMEM((rows, depth + 2 * HALO, cells), single),
                VMEM((rows, depth, LANES), single),
                VMEM((rows, depth, LANES), single),
                VMEM((HALO, depth, cells), single),
                VMEM((HALO, depth, cells), single),
                VMEM((rows, HALO, cells), single),
                VMEM((rows, HALO, cells), single),
                pltpu.SemaphoreType.DMA((2, 3, gz - 1)),
                pltpu.SemaphoreType.DMA((2, 3, gx - 1)),
                pltpu.SemaphoreType.DMA((2, 6)),
            ],
            compiler_params=pltpu.CompilerParams(
                collective_id=0, has_side_effects=True, vmem_limit_bytes=60 * 1024 * 1024
            ),
            name="section",
        )(
            seg_offset, seg_length, spectrum, theta, section_sum, stencil_index, stencil_weight,
            jnp.asarray(twist), jnp.asarray(np.concatenate([top, rest], axis=0)),
        )
    )


def solution(mesh):
    placed = (
        P(None, None, ("gy", "gx"), None, "gz"),
        P("gy", "gz", "gx"),
        P("gy", "gz", "gx"),
        P(),
        P(),
        P(),
        P(),
    )
    return jax.shard_map(
        body,
        mesh=mesh,
        in_specs=placed,
        out_specs=(P("gy", "gz", "gx"), P("gy", "gz", "gx")),
        check_vma=False,
    )
```

profile of v0, /device:TPU:0, one launch (start us, length us, event | category | flops | bytes accessed | tf_op | source)
XLA Modules:
  0.0 35.0 jit_solution(8525591264445359382)
XLA Ops:
  0.6 32.0 %section.1 = (f32[8,4,2048]{2,1,0:T(4,128)}, f32[8,4,2048]{2,1,0:T(4,128)}) custom-call(s32[4]{0:T(128)} %offset_ref.1, s32[4]{0:T(128)} %length_ref.1, f32[3,2,2,16,512]{4,3,2,1,0:T(8,128)} %spec_ref.1, f32[8,4,2048]{2,1,0:T(4,128)} %theta_ref.1, f32[8,4,2048]{2,1,0:T(4,128)} %sum_ref.1, s32[8,8192]{1,0:T(8,128)} %index_ref.1, f32[8,8192]{1,0:T(8,128)} %weight_ref.1, ...), custom_call_target="tpu_custom_call" | custom-call | tf_op jit(solution)/shard_map/section/pallas_call | solution.py:342
  32.6 0.0 copy-start
  32.6 1.7 %copy.13 = f32[8,4,2048]{2,1,0:T(4,128)} copy(f32[8,4,2048]{2,1,0:T(4,128)} %get-tuple-element.4) | data formatting | bytes 524288
  34.3 0.0 copy-done
  34.3 0.7 %copy.14 = f32[8,4,2048]{2,1,0:T(4,128)} copy(f32[8,4,2048]{2,1,0:T(4,128)S(1)} %copy-done) | data formatting | bytes 524288
Async XLA Ops:
  32.6 1.7 %copy-start = (f32[8,4,2048]{2,1,0:T(4,128)S(1)}, f32[8,4,2048]{2,1,0:T(4,128)}, u32[]{:S(2)}) copy-start(f32[8,4,2048]{2,1,0:T(4,128)} %get-tuple-element.5) | copy-start | bytes 786436
where the time goes:
time: 35.4 us; the launch traced here: 35 us
  Pallas kernels  32 us (90%)
  local copies, waits for them, and re-layouts  2.42 us (7%)
  between operations  0.65 us (2%)
    pallas_call x1, Pallas kernels, body(): pl.pallas_call(functools.partial(section_kernel, sizes, span), out_shape=...  32 us
    unnamed x4, local copies, waits for them, and re-layouts  2.42 us

commit v1 on v0

v1 whole, which is shorter than its diff:
```python
import functools
import math

import jax
import jax.numpy as jnp
import numpy as np
from jax import lax
from jax.experimental import pallas as pl
from jax.experimental.pallas import tpu as pltpu
from jax.sharding import PartitionSpec as P

MESH = pl.DeviceIdType.MESH
VMEM = pltpu.VMEM
LANES = 128
HALO = 4
TILE = 8
WIDTH = 512

first_coeffs = (0.8, -0.2, 4.0 / 105.0, -1.0 / 280.0)
second_coeffs = (1.6, -0.2, 8.0 / 315.0, -1.0 / 560.0)
center_coeff = -205.0 / 72.0
diffusivity = 0.15
time_step = 0.4
section_keep = -5.0 / 9.0
section_gain = 15.0 / 16.0


def whole_vmem(count):
    return [pl.BlockSpec(memory_space=VMEM)] * count


def rotate(value, turn):
    re, im = value
    cosine, sine = math.cos(2 * math.pi * turn), math.sin(2 * math.pi * turn)
    quarter = turn * 4 % 4
    if quarter == 0:
        return re, im
    if quarter == 1:
        return -im, re
    if quarter == 2:
        return -re, -im
    if quarter == 3:
        return im, -re
    return re * cosine - im * sine, re * sine + im * cosine


def fft(values):
    count = len(values)
    if count == 1:
        return values
    even = fft(values[0::2])
    odd = fft(values[1::2])
    low, high = [], []
    for x in range(count // 2):
        re, im = rotate(odd[x], x / count)
        low.append((even[x][0] + re, even[x][1] + im))
        high.append((even[x][0] - re, even[x][1] - im))
    return low + high


def split(value):
    top = value.astype(jnp.bfloat16)
    return top, (value - top.astype(jnp.float32)).astype(jnp.bfloat16)


def section_kernel(
    sizes, span,
    offset_ref, length_ref, spec_hbm, theta_hbm, sum_hbm, index_hbm, weight_hbm, twist_hbm, last_hbm,
    theta_out, sum_out,
    spec_ref, theta_ref, sum_ref, index_ref, weight_ref, twist_ref, last_ref,
    modes_send, modes_recv, mixed, velocity, seg_send, seg_recv, matrix_top, matrix_rest, gathered, values,
    grads, part, drift, field, z_back, z_front,
    load_sems, modes_sems, seg_sems, face_sems, deep_sems,
):
    gx, gy, gz = sizes
    here = {axis: lax.axis_index(axis) for axis in ("gx", "gy", "gz")}
    counts = dict(gx=gx, gy=gy, gz=gz)
    ahead = {axis: {axis: lax.rem(here[axis] + 1, counts[axis])} for axis in here}
    behind = {axis: {axis: lax.rem(here[axis] + counts[axis] - 1, counts[axis])} for axis in here}
    me, layer = here["gx"], here["gz"]
    rows, depth, cells = theta_ref.shape
    _, _, own_rows, all_depth, modes = spec_ref.shape
    local_slabs = modes // LANES
    group = own_rows * depth
    slabs = gz * local_slabs
    near = 2 * slabs
    far = 2 * slabs
    taps = index_ref.shape[0]
    lines = rows * depth
    tiles = lines // TILE
    skirt = HALO * depth

    own_columns = pl.ds(pl.multiple_of(me * cells, LANES), cells)
    loads = [
        pltpu.make_async_copy(source, place, load_sems.at[number])
        for number, (source, place) in enumerate(
            [
                (spec_hbm, spec_ref),
                (theta_hbm, theta_ref),
                (index_hbm.at[:, own_columns], index_ref),
                (weight_hbm.at[:, own_columns], weight_ref),
                (twist_hbm, twist_ref),
                (last_hbm, last_ref),
                (sum_hbm, sum_ref),
            ]
        )
    ]
    for load in loads:
        load.start()

    barrier = pltpu.get_barrier_semaphore()
    targets = [{"gx": lax.rem(me + step, gx)} for step in range(1, gx)]
    targets += [{"gz": lax.rem(layer + step, gz)} for step in range(1, gz)]
    targets += [ahead["gy"], behind["gy"]]
    for target in targets:
        pl.semaphore_signal(barrier, inc=1, device_id=target, device_id_type=MESH)

    loads[0].wait()
    for comp in range(3):
        for slab in range(local_slabs):
            for part_of in range(2):
                for row in range(own_rows):
                    held = spec_ref[comp, part_of, row, :, slab * LANES : (slab + 1) * LANES]
                    at = part_of * group + row * depth
                    for peer in range(gz):
                        modes_send[comp, peer, slab, at : at + depth, :] = held[
                            peer * depth : (peer + 1) * depth
                        ]
    pl.semaphore_wait(barrier, len(targets))

    def modes_copy(comp, target):
        return pltpu.make_async_remote_copy(
            src_ref=modes_send.at[comp, target],
            dst_ref=modes_recv.at[comp, layer],
            send_sem=modes_sems.at[0, comp, target],
            recv_sem=modes_sems.at[1, comp, layer],
            device_id={"gz": target},
            device_id_type=MESH,
        )

    def modes_wait(comp, other):
        pltpu.make_async_remote_copy(
            src_ref=modes_send.at[comp, other],
            dst_ref=modes_recv.at[comp, other],
            send_sem=modes_sems.at[0, comp, other],
            recv_sem=modes_sems.at[1, comp, other],
            device_id={"gz": other},
            device_id_type=MESH,
        ).wait()

    def send_modes(comp, distance):
        @pl.when(layer + distance < gz)
        def _():
            modes_copy(comp, layer + distance).start()

        @pl.when(layer >= distance)
        def _():
            modes_copy(comp, layer - distance).start()

    for comp in range(3):
        send_modes(comp, 1)
    for comp in range(3):
        for distance in range(2, gz):
            send_modes(comp, distance)

    def seg_copy(comp, step):
        target = lax.rem(me + step, gx)
        return pltpu.make_async_remote_copy(
            src_ref=seg_send.at[comp, target],
            dst_ref=seg_recv.at[comp, me],
            send_sem=seg_sems.at[0, comp, step - 1],
            recv_sem=seg_sems.at[1, comp, step - 1],
            device_id={"gx": target},
            device_id_type=MESH,
        )

    loads[1].wait()
    for tile in range(tiles):
        at = skirt + tile * TILE
        for half in range(TILE // depth):
            field[at + half * depth : at + (half + 1) * depth, LANES : LANES + cells] = theta_ref[
                tile * (TILE // depth) + half
            ]

    mine = pl.ds(skirt, lines)
    middle = pl.ds(LANES, cells)
    faces = [
        pltpu.make_async_remote_copy(
            src_ref=field.at[source],
            dst_ref=field.at[place],
            send_sem=face_sems.at[0, number],
            recv_sem=face_sems.at[1, number],
            device_id=device,
            device_id_type=MESH,
        )
        for number, (source, place, device) in enumerate(
            [
                ((mine, pl.ds(cells, LANES)), (mine, pl.ds(0, LANES)), ahead["gx"]),
                ((mine, pl.ds(LANES, LANES)), (mine, pl.ds(LANES + cells, LANES)), behind["gx"]),
                ((pl.ds(lines, skirt), middle), (pl.ds(0, skirt), middle), ahead["gy"]),
                ((pl.ds(skirt, skirt), middle), (pl.ds(skirt + lines, skirt), middle), behind["gy"]),
            ]
        )
    ]
    for face in faces:
        face.start()

    def deep_copy(way, tile):
        return pltpu.make_async_remote_copy(
            src_ref=field.at[pl.ds(skirt + tile * TILE, TILE), middle],
            dst_ref=(z_back, z_front)[way].at[pl.ds(tile * TILE, TILE)],
            send_sem=deep_sems.at[0, way, tile],
            recv_sem=deep_sems.at[1, way, tile],
            device_id=(ahead, behind)[way]["gz"],
            device_id_type=MESH,
        )

    for comp in range(3):
        modes_recv[comp, layer] = modes_send[comp, layer]

    loads[2].wait()
    loads[3].wait()
    live_count = length_ref[me]
    begin = offset_ref[me] - jnp.minimum(offset_ref[me] // LANES, far - span) * LANES
    counter = lax.broadcasted_iota(jnp.int32, (LANES, LANES), 0).astype(jnp.float32).astype(jnp.bfloat16)
    counters = [counter[step : step + 16] for step in range(0, LANES, 16)]

    def spread(row):
        return jnp.broadcast_to(row, (16, LANES)).astype(jnp.bfloat16)

    def build(chunk, carry):
        columns = pl.ds(pl.multiple_of(chunk * LANES, LANES), LANES)
        index = index_ref[:, columns]
        live = index < live_count
        weight = jnp.where(live, weight_ref[:, columns], 0.0)
        merged = jnp.zeros_like(weight)
        for tap in range(taps):
            merged = merged + jnp.where(index == index[tap : tap + 1], weight[tap : tap + 1], 0.0)
        high, low = split(merged)
        high, low = high.astype(jnp.float32), low.astype(jnp.float32)
        place = jnp.where(live, index + begin, -1)
        owner = (place >> 7).astype(jnp.float32)
        within = (place & (LANES - 1)).astype(jnp.float32)
        tops = [spread(high[tap : tap + 1]) for tap in range(taps)]
        rests = [spread(low[tap : tap + 1]) for tap in range(taps)]
        owners = [spread(owner[tap : tap + 1]) for tap in range(taps)]
        withins = [spread(within[tap : tap + 1]) for tap in range(taps)]

        def slab_of(slab, inner):
            number = jnp.full((16, LANES), slab, jnp.int32).astype(jnp.float32).astype(jnp.bfloat16)
            close = [
                jnp.where(owners[tap] == number, withins[tap], jnp.bfloat16(-1)) for tap in range(taps)
            ]
            for step in range(LANES // 16):
                top = jnp.zeros((16, LANES), jnp.bfloat16)
                rest = jnp.zeros((16, LANES), jnp.bfloat16)
                for tap in range(taps):
                    hit = counters[step] == close[tap]
                    top = jnp.where(hit, tops[tap], top)
                    rest = jnp.where(hit, rests[tap], rest)
                at = pl.ds(pl.multiple_of(slab * LANES + step * 16, 16), 16)
                matrix_top[chunk, at, :] = top
                matrix_rest[chunk, at, :] = rest
            return inner

        return lax.fori_loop(0, span, slab_of, carry)

    lax.fori_loop(0, cells // LANES, build, 0)

    @pl.when(layer == gz - 1)
    def _():
        for way in (1, 0):
            for tile in range(tiles):
                deep_copy(way, tile).start()

    @pl.when(layer != gz - 1)
    def _():
        for way in (0, 1):
            for tile in range(tiles):
                deep_copy(way, tile).start()

    loads[4].wait()
    loads[5].wait()
    last_both = last_ref[...]
    last_top = last_both[:far]
    dims = (((1,), (1,)), ((), ()))

    def twisted(line):
        re, im = mixed[:, line, :], mixed[:, group + line, :]
        pieces = []
        for quarter in range(LANES // near):
            part_of = slice(quarter * near, (quarter + 1) * near)
            cosine, sine = twist_ref[0, part_of, :], twist_ref[1, part_of, :]
            pieces.append(jnp.concatenate([re * cosine - im * sine, re * sine + im * cosine], axis=1))
        return jnp.concatenate(pieces, axis=0)

    def transform(comp, carry):
        for step in range(1, gz):
            modes_wait(comp, lax.rem(layer + step, gz))

        def arrived(k):
            held = modes_recv[comp, k // local_slabs, k % local_slabs]
            return held[:group], held[group:]

        for parity in range(2):
            mixes = fft([rotate(arrived(k), parity * k / near) for k in range(slabs)])
            for x in range(slabs):
                mixed[2 * x + parity, 0:group, :] = mixes[x][0]
                mixed[2 * x + parity, group:, :] = mixes[x][1]
        for pair in range(group // 2):
            turned = jnp.concatenate([twisted(2 * pair), twisted(2 * pair + 1)], axis=0)
            top, rest = split(turned)
            first = lax.dot_general(last_both, top, dims, preferred_element_type=jnp.float32)
            second = lax.dot_general(last_top, rest, dims, preferred_element_type=jnp.float32)
            total = first[:far] + (first[far:] + second)
            velocity[:, 2 * pair, :] = total[:, :LANES]
            velocity[:, 2 * pair + 1, :] = total[:, LANES:]
        for block in range(gx):
            start = jnp.minimum(offset_ref[block] // LANES, far - span)
            seg_send[comp, block] = velocity[pl.ds(start, span)]
        for step in range(1, gx):
            seg_copy(comp, step).start()
        seg_recv[comp, me] = seg_send[comp, me]
        return carry

    lax.fori_loop(0, 3, transform, 0)

    loads[6].wait()
    for tile in range(tiles):
        for half in range(TILE // depth):
            at = tile * TILE + half * depth
            part[at : at + depth, :] = section_keep * sum_ref[tile * (TILE // depth) + half]
    for face in faces:
        face.wait()
    width = min(WIDTH, cells)
    wide_width = width + 2 * LANES
    low_half = lax.broadcasted_iota(jnp.int32, (TILE, width), 0) < depth

    def plane(block, carry):
        columns = pl.ds(pl.multiple_of(block * width, LANES), width)
        inner = pl.ds(pl.multiple_of(block * width + LANES, LANES), width)
        around = pl.ds(pl.multiple_of(block * width, LANES), wide_width)
        for tile in range(tiles):
            stack = [field[(tile + step) * TILE : (tile + step + 1) * TILE, inner] for step in range(5)]
            turned = [pltpu.roll(held, depth, 0) for held in stack]
            between = [jnp.where(low_half, turned[step], turned[step + 1]) for step in range(4)]
            behind_y = [between[1], stack[1], between[0], stack[0]]
            ahead_y = [between[2], stack[3], between[3], stack[4]]
            wide = field[skirt + tile * TILE : skirt + (tile + 1) * TILE, around]
            grad_x = jnp.zeros((TILE, width), jnp.float32)
            grad_y = jnp.zeros((TILE, width), jnp.float32)
            partial = 3.0 * center_coeff * stack[2]
            for reach in range(1, 5):
                ahead_x = pltpu.roll(wide, wide_width - reach, 1)[:, LANES : LANES + width]
                behind_x = pltpu.roll(wide, reach, 1)[:, LANES : LANES + width]
                up, down = ahead_y[reach - 1], behind_y[reach - 1]
                grad_x = grad_x + first_coeffs[reach - 1] * (ahead_x - behind_x)
                grad_y = grad_y + first_coeffs[reach - 1] * (up - down)
                partial = partial + second_coeffs[reach - 1] * ((ahead_x + behind_x) + (up + down))
            at = slice(tile * TILE, (tile + 1) * TILE)
            grads[0, at, columns] = grad_x
            grads[1, at, columns] = grad_y
            part[at, columns] = part[at, columns] + (time_step * diffusivity) * partial
        return carry

    lax.fori_loop(0, cells // width, plane, 0)

    for comp in range(3):
        for step in range(1, gx):
            seg_copy(comp, step).wait()
    for comp in range(3):
        for block in range(gx):
            at = (comp * gx + block) * group
            for slab in range(span):
                gathered[at : at + group, slab * LANES : (slab + 1) * LANES] = seg_recv[comp, block, slab]
    total = 3 * lines
    top, rest = split(gathered[...])
    values[0:total, :] = top
    values[total:, :] = rest

    def combine(pair, carry):
        top = jnp.concatenate([matrix_top[2 * pair], matrix_top[2 * pair + 1]], axis=1)
        rest = jnp.concatenate([matrix_rest[2 * pair], matrix_rest[2 * pair + 1]], axis=1)
        first = jnp.dot(values[...], top, preferred_element_type=jnp.float32)
        second = jnp.dot(values[0:total, :], rest, preferred_element_type=jnp.float32)
        moved = first[:total] + (first[total:] + second)
        columns = pl.ds(pl.multiple_of(pair * 2 * LANES, 2 * LANES), 2 * LANES)
        carried = moved[:lines] * grads[0, :, columns] + moved[lines : 2 * lines] * grads[1, :, columns]
        part[:, columns] = part[:, columns] - time_step * carried
        drift[:, columns] = time_step * moved[2 * lines :]
        return carry

    lax.fori_loop(0, cells // (2 * LANES), combine, 0)

    place_of = lax.rem(lax.broadcasted_iota(jnp.int32, (TILE, width), 0), depth)
    for tile in range(tiles):
        for way in range(2):
            deep_copy(way, tile).wait()
        at = slice(tile * TILE, (tile + 1) * TILE)

        def finish(block, carry):
            columns = pl.ds(pl.multiple_of(block * width, LANES), width)
            inner = pl.ds(pl.multiple_of(block * width + LANES, LANES), width)
            own = field[skirt + tile * TILE : skirt + (tile + 1) * TILE, inner]
            back, front = z_back[at, columns], z_front[at, columns]
            grad_z = jnp.zeros((TILE, width), jnp.float32)
            partial = jnp.zeros((TILE, width), jnp.float32)
            for reach in range(1, 5):
                up, down = front, back
                if reach < HALO:
                    up = jnp.where(
                        place_of < depth - reach, pltpu.roll(own, TILE - reach, 0), pltpu.roll(front, depth - reach, 0)
                    )
                    down = jnp.where(
                        place_of >= reach, pltpu.roll(own, reach, 0), pltpu.roll(back, depth + reach, 0)
                    )
                grad_z = grad_z + first_coeffs[reach - 1] * (up - down)
                partial = partial + second_coeffs[reach - 1] * (up + down)
            after = (part[at, columns] + (time_step * diffusivity) * partial) - drift[at, columns] * grad_z
            later = own + section_gain * after
            for half in range(TILE // depth):
                row, piece = tile * (TILE // depth) + half, slice(half * depth, (half + 1) * depth)
                sum_out[row, :, columns] = after[piece]
                theta_out[row, :, columns] = later[piece]
            return carry

        lax.fori_loop(0, cells // width, finish, 0)


def put(theta_ref, sum_ref, theta_out, sum_out, sems):
    copies = [
        pltpu.make_async_copy(theta_ref, theta_out, sems.at[0]),
        pltpu.make_async_copy(sum_ref, sum_out, sems.at[1]),
    ]
    for copy in copies:
        copy.start()
    for copy in copies:
        copy.wait()


def body(spectrum, theta, section_sum, seg_offset, seg_length, stencil_index, stencil_weight):
    sizes = tuple(lax.axis_size(axis) for axis in ("gx", "gy", "gz"))
    gx, _, gz = sizes
    _, _, own_rows, all_depth, modes = spectrum.shape
    rows, depth, cells = theta.shape
    taps = stencil_index.shape[0]
    assert depth == HALO and rows * depth % TILE == 0 and cells % min(WIDTH, cells) == 0
    group = own_rows * depth
    slabs = gz * modes // LANES
    length = 2 * slabs * LANES
    far = length // LANES
    span = min(3 * length // (2 * gx) // LANES + 1, far)
    k = np.arange(LANES)
    turn = 2 * np.pi * (np.outer(k, k) % length) / length
    twist = np.stack([np.cos(turn), np.sin(turn)]).astype(np.float32)
    turn = 2 * np.pi * (np.outer(np.arange(far), k) % far) / far
    last = np.concatenate([np.cos(turn), -np.sin(turn)], axis=1).astype(np.float32)
    top = last.astype(jnp.bfloat16)
    rest = (last - top.astype(np.float32)).astype(jnp.bfloat16)
    modes_shape = (3, gz, modes // LANES, 2 * group, LANES)
    seg_shape = (3, gx, span, group, LANES)
    lines = rows * depth
    tiles = lines // TILE
    single = jnp.float32
    held = pl.pallas_call(
        functools.partial(section_kernel, sizes, span),
        out_shape=[VMEM(theta.shape, single)] * 2,
        in_specs=[pl.BlockSpec(memory_space=pltpu.SMEM)] * 2 + [pl.BlockSpec(memory_space=pltpu.HBM)] * 7,
        out_specs=whole_vmem(2),
        scratch_shapes=[
            VMEM(spectrum.shape, single),
            VMEM(theta.shape, single),
            VMEM(theta.shape, single),
            VMEM((taps, cells), jnp.int32),
            VMEM((taps, cells), single),
            VMEM(twist.shape, single),
            VMEM((2 * far, 2 * LANES), jnp.bfloat16),
            VMEM(modes_shape, single),
            VMEM(modes_shape, single),
            VMEM((2 * slabs, 2 * group, LANES), single),
            VMEM((far, group, LANES), single),
            VMEM(seg_shape, single),
            VMEM(seg_shape, single),
            VMEM((cells // LANES, span * LANES, LANES), jnp.bfloat16),
            VMEM((cells // LANES, span * LANES, LANES), jnp.bfloat16),
            VMEM((3 * lines, span * LANES), single),
            VMEM((6 * lines, span * LANES), jnp.bfloat16),
            VMEM((2, lines, cells), single),
            VMEM((lines, cells), single),
            VMEM((lines, cells), single),
            VMEM((lines + 2 * HALO * depth, cells + 2 * LANES), single),
            VMEM((lines, cells), single),
            VMEM((lines, cells), single),
            pltpu.SemaphoreType.DMA((7,)),
            pltpu.SemaphoreType.DMA((2, 3, gz)),
            pltpu.SemaphoreType.DMA((2, 3, gx - 1)),
            pltpu.SemaphoreType.DMA((2, 4)),
            pltpu.SemaphoreType.DMA((2, 2, tiles)),
        ],
        compiler_params=pltpu.CompilerParams(
            collective_id=0, has_side_effects=True, vmem_limit_bytes=40 * 1024 * 1024
        ),
        name="section",
    )(
        seg_offset, seg_length, spectrum, theta, section_sum, stencil_index, stencil_weight,
        jnp.asarray(twist), jnp.asarray(np.concatenate([top, rest], axis=0)),
    )
    return tuple(
        pl.pallas_call(
            put,
            out_shape=[jax.ShapeDtypeStruct(theta.shape, single)] * 2,
            in_specs=whole_vmem(2),
            out_specs=[pl.BlockSpec(memory_space=pltpu.HBM)] * 2,
            scratch_shapes=[pltpu.SemaphoreType.DMA((2,))],
            name="put",
        )(*held)
    )


def solution(mesh):
    placed = (
        P(None, None, ("gy", "gx"), None, "gz"),
        P("gy", "gz", "gx"),
        P("gy", "gz", "gx"),
        P(),
        P(),
        P(),
        P(),
    )
    return jax.shard_map(
        body,
        mesh=mesh,
        in_specs=placed,
        out_specs=(P("gy", "gz", "gx"), P("gy", "gz", "gx")),
        check_vma=False,
    )
```

time: 35.4 us -> 42 us (1.19)
  local copies, waits for them, and re-layouts: 2.42 us -> 9.15 us
    unnamed x4 -> x22, local copies, waits for them, and re-layouts: 2.42 us -> 9.15 us
    pallas_call x1, Pallas kernels: 32 us -> 30 us  [body(): pl.pallas_call(functools.partial(section_kernel, sizes, span), out_shape=...]
    pallas_call x0 -> x1, Pallas kernels: none -> 1.83 us  [body(): pl.pallas_call(put, out_shape=[jax.ShapeDtypeStruct(theta.shape, single)]...]
where the time goes in v1:
time: 42 us; the launch traced here: 41.6 us
  Pallas kernels  31.8 us (76%)
  local copies, waits for them, and re-layouts  9.15 us (22%)
  between operations  0.67 us (2%)
    pallas_call x1, Pallas kernels, body(): pl.pallas_call(functools.partial(section_kernel, sizes, span), out_shape=...  30 us
    unnamed x22, local copies, waits for them, and re-layouts  9.15 us
    pallas_call x1, Pallas kernels, body(): pl.pallas_call(put, out_shape=[jax.ShapeDtypeStruct(theta.shape, single)]...  1.83 us

profile of v1, /device:TPU:0, one launch (start us, length us, event | category | flops | bytes accessed | tf_op | source)
XLA Modules:
  0.0 41.6 jit_solution(10403676683097622101)
XLA Ops:
  0.6 0.0 copy-start
  0.6 1.0 %copy-done = f32[3,2,2,16,512]{4,3,2,1,0:T(8,128)S(1)} copy-done((f32[3,2,2,16,512]{4,3,2,1,0:T(8,128)S(1)}, f32[3,2,2,16,512]{4,3,2,1,0:T(8,128)}, u32[]{:S(2)}) %copy-start) | copy-done | bytes 393240
  1.6 0.0 copy-start.3
  1.6 0.9 %copy-done.3 = f32[8,4,2048]{2,1,0:T(4,128)S(1)} copy-done((f32[8,4,2048]{2,1,0:T(4,128)S(1)}, f32[8,4,2048]{2,1,0:T(4,128)}, u32[]{:S(2)}) %copy-start.3) | copy-done | bytes 262168
  2.6 0.0 copy-start.4
  2.6 0.9 %copy-done.4 = f32[8,4,2048]{2,1,0:T(4,128)S(1)} copy-done((f32[8,4,2048]{2,1,0:T(4,128)S(1)}, f32[8,4,2048]{2,1,0:T(4,128)}, u32[]{:S(2)}) %copy-start.4) | copy-done | bytes 262168
  3.5 0.0 copy-start.5
  3.5 0.9 %copy-done.5 = s32[8,8192]{1,0:T(8,128)S(1)} copy-done((s32[8,8192]{1,0:T(8,128)S(1)}, s32[8,8192]{1,0:T(8,128)}, u32[]{:S(2)}) %copy-start.5) | copy-done | bytes 262168
  4.5 0.0 copy-start.6
  4.5 0.9 %copy-done.6 = f32[8,8192]{1,0:T(8,128)S(1)} copy-done((f32[8,8192]{1,0:T(8,128)S(1)}, f32[8,8192]{1,0:T(8,128)}, u32[]{:S(2)}) %copy-start.6) | copy-done | bytes 262168
  5.4 0.0 copy-start.7
  5.4 0.9 %copy-done.7 = f32[2,128,128]{2,1,0:T(8,128)S(1)} copy-done((f32[2,128,128]{2,1,0:T(8,128)S(1)}, f32[2,128,128]{2,1,0:T(8,128)}, u32[]{:S(2)}) %copy-start.7) | copy-done | bytes 131096
  6.3 0.0 copy-start.8
  6.3 0.8 %copy-done.8 = bf16[64,256]{1,0:T(8,128)(2,1)S(1)} copy-done((bf16[64,256]{1,0:T(8,128)(2,1)S(1)}, bf16[64,256]{1,0:T(8,128)(2,1)}, u32[]{:S(2)}) %copy-start.8) | copy-done | bytes 32792
  7.1 0.0 copy-start.9
  7.1 0.7 %copy-done.9 = s32[4]{0:T(128)S(1)} copy-done((s32[4]{0:T(128)S(1)}, s32[4]{0:T(128)}, u32[]{:S(2)}) %copy-start.9) | copy-done | bytes 40
  7.8 0.0 copy-start.10
  7.8 0.7 %copy-done.10 = s32[4]{0:T(128)S(1)} copy-done((s32[4]{0:T(128)S(1)}, s32[4]{0:T(128)}, u32[]{:S(2)}) %copy-start.10) | copy-done | bytes 40
  8.4 30.0 %section.1 = (f32[8,4,2048]{2,1,0:T(4,128)S(1)}, f32[8,4,2048]{2,1,0:T(4,128)S(1)}) custom-call(s32[4]{0:T(128)S(1)} %copy-done.9, s32[4]{0:T(128)S(1)} %copy-done.10, f32[3,2,2,16,512]{4,3,2,1,0:T(8,128)S(1)} %copy-done, f32[8,4,2048]{2,1,0:T(4,128)S(1)} %copy-done.3, f32[8,4,2048]{2,1,0:T(4,128)S(1)} %copy-done.4, s32[8,8192]{1,0:T(8,128)S(1)} %copy-done.5, ...), custom_call_target="tpu_custom_call" | custom-call | tf_op jit(solution)/shard_map/section/pallas_call | solution.py:465
  38.4 0.0 copy-start.1
  38.4 0.7 %copy-done.1 = f32[8,4,2048]{2,1,0:T(4,128)} copy-done((f32[8,4,2048]{2,1,0:T(4,128)}, f32[8,4,2048]{2,1,0:T(4,128)S(1)}, u32[]{:S(2)}) %copy-start.1) | copy-done | bytes 262168
  39.1 0.0 copy-start.2
  39.1 0.7 %copy-done.2 = f32[8,4,2048]{2,1,0:T(4,128)} copy-done((f32[8,4,2048]{2,1,0:T(4,128)}, f32[8,4,2048]{2,1,0:T(4,128)S(1)}, u32[]{:S(2)}) %copy-start.2) | copy-done | bytes 262168
  39.8 1.8 %put.1 = (f32[8,4,2048]{2,1,0:T(4,128)}, f32[8,4,2048]{2,1,0:T(4,128)}) custom-call(f32[8,4,2048]{2,1,0:T(4,128)} %copy-done.1, f32[8,4,2048]{2,1,0:T(4,128)} %copy-done.2), custom_call_target="tpu_custom_call" | custom-call | tf_op jit(solution)/shard_map/put/pallas_call | solution.py:509
Async XLA Ops:
  0.6 1.0 %copy-start = (f32[3,2,2,16,512]{4,3,2,1,0:T(8,128)S(1)}, f32[3,2,2,16,512]{4,3,2,1,0:T(8,128)}, u32[]{:S(2)}) copy-start(f32[3,2,2,16,512]{4,3,2,1,0:T(8,128)} %spec_hbm.1) | copy-start | bytes 1179652
  1.6 0.9 %copy-start.3 = (f32[8,4,2048]{2,1,0:T(4,128)S(1)}, f32[8,4,2048]{2,1,0:T(4,128)}, u32[]{:S(2)}) copy-start(f32[8,4,2048]{2,1,0:T(4,128)} %theta_hbm.1) | copy-start | bytes 786436
  2.6 0.9 %copy-start.4 = (f32[8,4,2048]{2,1,0:T(4,128)S(1)}, f32[8,4,2048]{2,1,0:T(4,128)}, u32[]{:S(2)}) copy-start(f32[8,4,2048]{2,1,0:T(4,128)} %sum_hbm.1) | copy-start | bytes 786436
  3.5 0.9 %copy-start.5 = (s32[8,8192]{1,0:T(8,128)S(1)}, s32[8,8192]{1,0:T(8,128)}, u32[]{:S(2)}) copy-start(s32[8,8192]{1,0:T(8,128)} %index_hbm.1) | copy-start | bytes 786436
  4.5 0.9 %copy-start.6 = (f32[8,8192]{1,0:T(8,128)S(1)}, f32[8,8192]{1,0:T(8,128)}, u32[]{:S(2)}) copy-start(f32[8,8192]{1,0:T(8,128)} %weight_hbm.1) | copy-start | bytes 786436
  5.4 0.9 %copy-start.7 = (f32[2,128,128]{2,1,0:T(8,128)S(1)}, f32[2,128,128]{2,1,0:T(8,128)}, u32[]{:S(2)}) copy-start(f32[2,128,128]{2,1,0:T(8,128)} %constant.4.clone.twist_hbm) | copy-start | bytes 393220
  6.3 0.8 %copy-start.8 = (bf16[64,256]{1,0:T(8,128)(2,1)S(1)}, bf16[64,256]{1,0:T(8,128)(2,1)}, u32[]{:S(2)}) copy-start(bf16[64,256]{1,0:T(8,128)(2,1)} %constant.5.clone.last_hbm) | copy-start | bytes 98308
  7.1 0.7 %copy-start.9 = (s32[4]{0:T(128)S(1)}, s32[4]{0:T(128)}, u32[]{:S(2)}) copy-start(s32[4]{0:T(128)} %offset_ref.1) | copy-start | bytes 52
  7.8 0.7 %copy-start.10 = (s32[4]{0:T(128)S(1)}, s32[4]{0:T(128)}, u32[]{:S(2)}) copy-start(s32[4]{0:T(128)} %length_ref.1) | copy-start | bytes 52
  38.4 0.7 %copy-start.1 = (f32[8,4,2048]{2,1,0:T(4,128)}, f32[8,4,2048]{2,1,0:T(4,128)S(1)}, u32[]{:S(2)}) copy-start(f32[8,4,2048]{2,1,0:T(4,128)S(1)} %get-tuple-element.4.theta_ref) | copy-start | bytes 786436
  39.1 0.7 %copy-start.2 = (f32[8,4,2048]{2,1,0:T(4,128)}, f32[8,4,2048]{2,1,0:T(4,128)S(1)}, u32[]{:S(2)}) copy-start(f32[8,4,2048]{2,1,0:T(4,128)S(1)} %get-tuple-element.5.sum_ref) | copy-start | bytes 786436

commit v2 on v1

--- a/solution.py
+++ b/solution.py
@@ -498,7 +498,7 @@
             pltpu.SemaphoreType.DMA((2, 2, tiles)),
         ],
         compiler_params=pltpu.CompilerParams(
-            collective_id=0, has_side_effects=True, vmem_limit_bytes=40 * 1024 * 1024
+            collective_id=0, has_side_effects=True, vmem_limit_bytes=60 * 1024 * 1024
         ),
         name="section",
     )(
@@ -509,9 +509,10 @@
         pl.pallas_call(
             put,
             out_shape=[jax.ShapeDtypeStruct(theta.shape, single)] * 2,
-            in_specs=whole_vmem(2),
+            in_specs=[pl.BlockSpec(memory_space=pl.ANY)] * 2,
             out_specs=[pl.BlockSpec(memory_space=pltpu.HBM)] * 2,
             scratch_shapes=[pltpu.SemaphoreType.DMA((2,))],
+            compiler_params=pltpu.CompilerParams(vmem_limit_bytes=1024 * 1024),
             name="put",
         )(*held)
     )

time: 42 us -> 31.1 us (0.74)
  local copies, waits for them, and re-layouts: 9.15 us -> 0 us
  Pallas kernels: 31.8 us -> 30.3 us
    unnamed x22 -> x0, local copies, waits for them, and re-layouts: 9.15 us -> none
    pallas_call x1, Pallas kernels: 1.83 us -> 0.81 us  [body(): pl.pallas_call(put, out_shape=[jax.ShapeDtypeStruct(theta.shape, single)]...]
    pallas_call x1, Pallas kernels: 30 us -> 29.5 us  [body(): pl.pallas_call(functools.partial(section_kernel, sizes, span), out_shape=...]
where the time goes in v2:
time: 31.1 us; the launch traced here: 31 us
  Pallas kernels  30.3 us (97%)
  between operations  0.64 us (2%)
    pallas_call x1, Pallas kernels, body(): pl.pallas_call(functools.partial(section_kernel, sizes, span), out_shape=...  29.5 us
    pallas_call x1, Pallas kernels, body(): pl.pallas_call(put, out_shape=[jax.ShapeDtypeStruct(theta.shape, single)]...  0.81 us

profile of v2, /device:TPU:0, one launch (start us, length us, event | category | flops | bytes accessed | tf_op | source)
XLA Modules:
  0.0 31.0 jit_solution(12038738724136353795)
XLA Ops:
  0.6 29.5 %section.1 = (f32[8,4,2048]{2,1,0:T(4,128)S(1)}, f32[8,4,2048]{2,1,0:T(4,128)S(1)}) custom-call(s32[4]{0:T(128)} %offset_ref.1, s32[4]{0:T(128)} %length_ref.1, f32[3,2,2,16,512]{4,3,2,1,0:T(8,128)} %spec_hbm.1, f32[8,4,2048]{2,1,0:T(4,128)} %theta_hbm.1, f32[8,4,2048]{2,1,0:T(4,128)} %sum_hbm.1, s32[8,8192]{1,0:T(8,128)} %index_hbm.1, ...), custom_call_target="tpu_custom_call" | custom-call | tf_op jit(solution)/shard_map/section/pallas_call | solution.py:465
  30.2 0.8 %put.1 = (f32[8,4,2048]{2,1,0:T(4,128)}, f32[8,4,2048]{2,1,0:T(4,128)}) custom-call(f32[8,4,2048]{2,1,0:T(4,128)S(1)} %get-tuple-element.4.theta_ref, f32[8,4,2048]{2,1,0:T(4,128)S(1)} %get-tuple-element.5.sum_ref), custom_call_target="tpu_custom_call" | custom-call | tf_op jit(solution)/shard_map/put/pallas_call | solution.py:509

commit v3 on v2

--- a/solution.py
+++ b/solution.py
@@ -70,7 +70,7 @@
     spec_ref, theta_ref, sum_ref, index_ref, weight_ref, twist_ref, last_ref,
     modes_send, modes_recv, mixed, velocity, seg_send, seg_recv, matrix_top, matrix_rest, gathered, values,
     grads, part, drift, field, z_back, z_front,
-    load_sems, modes_sems, seg_sems, face_sems, deep_sems,
+    load_sems, modes_sems, seg_sems, face_sems, deep_sems, relay_sems,
 ):
     gx, gy, gz = sizes
     here = {axis: lax.axis_index(axis) for axis in ("gx", "gy", "gz")}
@@ -109,11 +109,23 @@
         load.start()
 
     barrier = pltpu.get_barrier_semaphore()
+    has_up, has_down = layer < gz - 1, layer > 0
+
+    def signal(semaphore, target):
+        pl.semaphore_signal(semaphore, inc=1, device_id=target, device_id_type=MESH)
+
+    @pl.when(has_up)
+    def _():
+        signal(barrier, {"gz": layer + 1})
+
+    @pl.when(has_down)
+    def _():
+        signal(barrier, {"gz": layer - 1})
+
     targets = [{"gx": lax.rem(me + step, gx)} for step in range(1, gx)]
-    targets += [{"gz": lax.rem(layer + step, gz)} for step in range(1, gz)]
     targets += [ahead["gy"], behind["gy"]]
     for target in targets:
-        pl.semaphore_signal(barrier, inc=1, device_id=target, device_id_type=MESH)
+        signal(barrier, target)
 
     loads[0].wait()
     for comp in range(3):
@@ -126,7 +138,32 @@
                         modes_send[comp, peer, slab, at : at + depth, :] = held[
                             peer * depth : (peer + 1) * depth
                         ]
-    pl.semaphore_wait(barrier, len(targets))
+
+    @pl.when(jnp.logical_and(has_up, has_down))
+    def _():
+        pl.semaphore_wait(barrier, len(targets) + 2)
+
+    @pl.when(jnp.logical_not(jnp.logical_and(has_up, has_down)))
+    def _():
+        pl.semaphore_wait(barrier, len(targets) + 1)
+
+    def tell(distance):
+        @pl.when(jnp.logical_and(has_down, layer + distance - 1 < gz))
+        def _():
+            signal(relay_sems.at[0, distance], {"gz": layer - 1})
+
+        @pl.when(jnp.logical_and(has_up, layer >= distance - 1))
+        def _():
+            signal(relay_sems.at[1, distance], {"gz": layer + 1})
+
+    def hear(distance):
+        @pl.when(layer + distance < gz)
+        def _():
+            pl.semaphore_wait(relay_sems.at[0, distance], 1)
+
+        @pl.when(layer >= distance)
+        def _():
+            pl.semaphore_wait(relay_sems.at[1, distance], 1)
 
     def modes_copy(comp, target):
         return pltpu.make_async_remote_copy(
@@ -157,9 +194,16 @@
         def _():
             modes_copy(comp, layer - distance).start()
 
+    if gz > 2:
+        tell(2)
     for comp in range(3):
         send_modes(comp, 1)
-    for comp in range(3):
+    for distance in range(2, gz):
+        hear(distance)
+        if distance + 1 < gz:
+            tell(distance + 1)
+        send_modes(0, distance)
+    for comp in range(1, 3):
         for distance in range(2, gz):
             send_modes(comp, distance)
 
@@ -265,7 +309,9 @@
 
         return lax.fori_loop(0, span, slab_of, carry)
 
-    lax.fori_loop(0, cells // LANES, build, 0)
+    chunks = cells // LANES
+    early, step_of = chunks * 3 // 8, chunks // 8
+    lax.fori_loop(0, early, build, 0)
 
     @pl.when(layer == gz - 1)
     def _():
@@ -295,6 +341,7 @@
         return jnp.concatenate(pieces, axis=0)
 
     def transform(comp, carry):
+        lax.fori_loop(early + comp * step_of, early + (comp + 1) * step_of, build, 0)
         for step in range(1, gz):
             modes_wait(comp, lax.rem(layer + step, gz))
 
@@ -324,6 +371,7 @@
         return carry
 
     lax.fori_loop(0, 3, transform, 0)
+    lax.fori_loop(early + 3 * step_of, chunks, build, 0)
 
     loads[6].wait()
     for tile in range(tiles):
@@ -496,6 +544,7 @@
             pltpu.SemaphoreType.DMA((2, 3, gx - 1)),
             pltpu.SemaphoreType.DMA((2, 4)),
             pltpu.SemaphoreType.DMA((2, 2, tiles)),
+            pltpu.SemaphoreType.REGULAR((2, gz)),
         ],
         compiler_params=pltpu.CompilerParams(
             collective_id=0, has_side_effects=True, vmem_limit_bytes=60 * 1024 * 1024

time: 31.1 us -> 30.4 us (0.977)
  Pallas kernels: 30.3 us -> 29.6 us
    pallas_call x1, Pallas kernels: 29.5 us -> 28.8 us  [body(): pl.pallas_call(functools.partial(section_kernel, sizes, span), out_shape=...]
where the time goes in v3:
time: 30.4 us; the launch traced here: 30.2 us
  Pallas kernels  29.6 us (97%)
  between operations  0.64 us (2%)
    pallas_call x1, Pallas kernels, body(): pl.pallas_call(functools.partial(section_kernel, sizes, span), out_shape=...  28.8 us
    pallas_call x1, Pallas kernels, body(): pl.pallas_call(put, out_shape=[jax.ShapeDtypeStruct(theta.shape, single)]...  0.81 us

profile of v3, /device:TPU:0, one launch (start us, length us, event | category | flops | bytes accessed | tf_op | source)
XLA Modules:
  0.0 30.2 jit_solution(15198680474082832490)
XLA Ops:
  0.6 28.8 %section.1 = (f32[8,4,2048]{2,1,0:T(4,128)S(1)}, f32[8,4,2048]{2,1,0:T(4,128)S(1)}) custom-call(s32[4]{0:T(128)} %offset_ref.1, s32[4]{0:T(128)} %length_ref.1, f32[3,2,2,16,512]{4,3,2,1,0:T(8,128)} %spec_hbm.1, f32[8,4,2048]{2,1,0:T(4,128)} %theta_hbm.1, f32[8,4,2048]{2,1,0:T(4,128)} %sum_hbm.1, s32[8,8192]{1,0:T(8,128)} %index_hbm.1, ...), custom_call_target="tpu_custom_call" | custom-call | tf_op jit(solution)/shard_map/section/pallas_call | solution.py:513
  29.4 0.8 %put.1 = (f32[8,4,2048]{2,1,0:T(4,128)}, f32[8,4,2048]{2,1,0:T(4,128)}) custom-call(f32[8,4,2048]{2,1,0:T(4,128)S(1)} %get-tuple-element.4.theta_ref, f32[8,4,2048]{2,1,0:T(4,128)S(1)} %get-tuple-element.5.sum_ref), custom_call_target="tpu_custom_call" | custom-call | tf_op jit(solution)/shard_map/put/pallas_call | solution.py:558

commit v4 on v2

--- a/solution.py
+++ b/solution.py
@@ -95,7 +95,9 @@
         pltpu.make_async_copy(source, place, load_sems.at[number])
         for number, (source, place) in enumerate(
             [
-                (spec_hbm, spec_ref),
+                (spec_hbm.at[0], spec_ref.at[0]),
+                (spec_hbm.at[1], spec_ref.at[1]),
+                (spec_hbm.at[2], spec_ref.at[2]),
                 (theta_hbm, theta_ref),
                 (index_hbm.at[:, own_columns], index_ref),
                 (weight_hbm.at[:, own_columns], weight_ref),
@@ -109,14 +111,74 @@
         load.start()
 
     barrier = pltpu.get_barrier_semaphore()
+    has_up, has_down = layer < gz - 1, layer > 0
+    inner = jnp.logical_and(has_up, has_down)
+    per_tile = TILE // depth
+
+    def signal(semaphore, target):
+        pl.semaphore_signal(semaphore, inc=1, device_id=target, device_id_type=MESH)
+
     targets = [{"gx": lax.rem(me + step, gx)} for step in range(1, gx)]
     targets += [{"gz": lax.rem(layer + step, gz)} for step in range(1, gz)]
     targets += [ahead["gy"], behind["gy"]]
     for target in targets:
-        pl.semaphore_signal(barrier, inc=1, device_id=target, device_id_type=MESH)
-
-    loads[0].wait()
+        signal(barrier, target)
+
+    pl.semaphore_wait(barrier, len(targets))
+
+    def modes_copy(comp, target):
+        return pltpu.make_async_remote_copy(
+            src_ref=modes_send.at[comp, target],
+            dst_ref=modes_recv.at[comp, layer],
+            send_sem=modes_sems.at[0, comp, target],
+            recv_sem=modes_sems.at[1, comp, layer],
+            device_id={"gz": target},
+            device_id_type=MESH,
+        )
+
+    def modes_wait(comp, other):
+        pltpu.make_async_remote_copy(
+            src_ref=modes_send.at[comp, other],
+            dst_ref=modes_recv.at[comp, other],
+            send_sem=modes_sems.at[0, comp, other],
+            recv_sem=modes_sems.at[1, comp, other],
+            device_id={"gz": other},
+            device_id_type=MESH,
+        ).wait()
+
+    def send_modes(comp, distance):
+        @pl.when(layer + distance < gz)
+        def _():
+            modes_copy(comp, layer + distance).start()
+
+        @pl.when(layer >= distance)
+        def _():
+            modes_copy(comp, layer - distance).start()
+
+    def deep_copy(way, tile):
+        part_of = pl.ds(tile * per_tile, per_tile)
+        return pltpu.make_async_remote_copy(
+            src_ref=theta_hbm.at[part_of],
+            dst_ref=(z_back, z_front)[way].at[part_of],
+            send_sem=deep_sems.at[0, way, tile],
+            recv_sem=deep_sems.at[1, way, tile],
+            device_id=(ahead, behind)[way]["gz"],
+            device_id_type=MESH,
+        )
+
+    def send_near(chosen):
+        @pl.when(has_up)
+        def _():
+            for tile in chosen:
+                deep_copy(0, tile).start()
+
+        @pl.when(has_down)
+        def _():
+            for tile in chosen:
+                deep_copy(1, tile).start()
+
     for comp in range(3):
+        loads[comp].wait()
         for slab in range(local_slabs):
             for part_of in range(2):
                 for row in range(own_rows):
@@ -126,42 +188,21 @@
                         modes_send[comp, peer, slab, at : at + depth, :] = held[
                             peer * depth : (peer + 1) * depth
                         ]
-    pl.semaphore_wait(barrier, len(targets))
-
-    def modes_copy(comp, target):
-        return pltpu.make_async_remote_copy(
-            src_ref=modes_send.at[comp, target],
-            dst_ref=modes_recv.at[comp, layer],
-            send_sem=modes_sems.at[0, comp, target],
-            recv_sem=modes_sems.at[1, comp, layer],
-            device_id={"gz": target},
-            device_id_type=MESH,
-        )
-
-    def modes_wait(comp, other):
-        pltpu.make_async_remote_copy(
-            src_ref=modes_send.at[comp, other],
-            dst_ref=modes_recv.at[comp, other],
-            send_sem=modes_sems.at[0, comp, other],
-            recv_sem=modes_sems.at[1, comp, other],
-            device_id={"gz": other},
-            device_id_type=MESH,
-        ).wait()
-
-    def send_modes(comp, distance):
-        @pl.when(layer + distance < gz)
+        for distance in range(gz - 1, 0, -1):
+            send_modes(comp, distance)
+    send_near(range(tiles))
+
+    @pl.when(jnp.logical_not(inner))
+    def _():
+        @pl.when(jnp.logical_not(has_up))
         def _():
-            modes_copy(comp, layer + distance).start()
-
-        @pl.when(layer >= distance)
+            for tile in range(tiles):
+                deep_copy(0, tile).start()
+
+        @pl.when(jnp.logical_not(has_down))
         def _():
-            modes_copy(comp, layer - distance).start()
-
-    for comp in range(3):
-        send_modes(comp, 1)
-    for comp in range(3):
-        for distance in range(2, gz):
-            send_modes(comp, distance)
+            for tile in range(tiles):
+                deep_copy(1, tile).start()
 
     def seg_copy(comp, step):
         target = lax.rem(me + step, gx)
@@ -174,12 +215,12 @@
             device_id_type=MESH,
         )
 
-    loads[1].wait()
+    loads[3].wait()
     for tile in range(tiles):
         at = skirt + tile * TILE
-        for half in range(TILE // depth):
+        for half in range(per_tile):
             field[at + half * depth : at + (half + 1) * depth, LANES : LANES + cells] = theta_ref[
-                tile * (TILE // depth) + half
+                tile * (per_tile) + half
             ]
 
     mine = pl.ds(skirt, lines)
@@ -205,21 +246,11 @@
     for face in faces:
         face.start()
 
-    def deep_copy(way, tile):
-        return pltpu.make_async_remote_copy(
-            src_ref=field.at[pl.ds(skirt + tile * TILE, TILE), middle],
-            dst_ref=(z_back, z_front)[way].at[pl.ds(tile * TILE, TILE)],
-            send_sem=deep_sems.at[0, way, tile],
-            recv_sem=deep_sems.at[1, way, tile],
-            device_id=(ahead, behind)[way]["gz"],
-            device_id_type=MESH,
-        )
-
     for comp in range(3):
         modes_recv[comp, layer] = modes_send[comp, layer]
 
-    loads[2].wait()
-    loads[3].wait()
+    loads[4].wait()
+    loads[5].wait()
     live_count = length_ref[me]
     begin = offset_ref[me] - jnp.minimum(offset_ref[me] // LANES, far - span) * LANES
     counter = lax.broadcasted_iota(jnp.int32, (LANES, LANES), 0).astype(jnp.float32).astype(jnp.bfloat16)
@@ -265,22 +296,12 @@
 
         return lax.fori_loop(0, span, slab_of, carry)
 
-    lax.fori_loop(0, cells // LANES, build, 0)
-
-    @pl.when(layer == gz - 1)
-    def _():
-        for way in (1, 0):
-            for tile in range(tiles):
-                deep_copy(way, tile).start()
-
-    @pl.when(layer != gz - 1)
-    def _():
-        for way in (0, 1):
-            for tile in range(tiles):
-                deep_copy(way, tile).start()
-
-    loads[4].wait()
-    loads[5].wait()
+    chunks = cells // LANES
+    early, step_of = chunks * 3 // 8, chunks // 8
+    lax.fori_loop(0, early, build, 0)
+
+    loads[6].wait()
+    loads[7].wait()
     last_both = last_ref[...]
     last_top = last_both[:far]
     dims = (((1,), (1,)), ((), ()))
@@ -295,6 +316,7 @@
         return jnp.concatenate(pieces, axis=0)
 
     def transform(comp, carry):
+        lax.fori_loop(early + comp * step_of, early + (comp + 1) * step_of, build, 0)
         for step in range(1, gz):
             modes_wait(comp, lax.rem(layer + step, gz))
 
@@ -324,12 +346,13 @@
         return carry
 
     lax.fori_loop(0, 3, transform, 0)
-
-    loads[6].wait()
+    lax.fori_loop(early + 3 * step_of, chunks, build, 0)
+
+    loads[8].wait()
     for tile in range(tiles):
-        for half in range(TILE // depth):
+        for half in range(per_tile):
             at = tile * TILE + half * depth
-            part[at : at + depth, :] = section_keep * sum_ref[tile * (TILE // depth) + half]
+            part[at : at + depth, :] = section_keep * sum_ref[tile * (per_tile) + half]
     for face in faces:
         face.wait()
     width = min(WIDTH, cells)
@@ -402,7 +425,10 @@
             columns = pl.ds(pl.multiple_of(block * width, LANES), width)
             inner = pl.ds(pl.multiple_of(block * width + LANES, LANES), width)
             own = field[skirt + tile * TILE : skirt + (tile + 1) * TILE, inner]
-            back, front = z_back[at, columns], z_front[at, columns]
+            back, front = (
+                jnp.concatenate([held[tile * per_tile + half, :, columns] for half in range(per_tile)], axis=0)
+                for held in (z_back, z_front)
+            )
             grad_z = jnp.zeros((TILE, width), jnp.float32)
             partial = jnp.zeros((TILE, width), jnp.float32)
             for reach in range(1, 5):
@@ -418,8 +444,8 @@
                 partial = partial + second_coeffs[reach - 1] * (up + down)
             after = (part[at, columns] + (time_step * diffusivity) * partial) - drift[at, columns] * grad_z
             later = own + section_gain * after
-            for half in range(TILE // depth):
-                row, piece = tile * (TILE // depth) + half, slice(half * depth, (half + 1) * depth)
+            for half in range(per_tile):
+                row, piece = tile * (per_tile) + half, slice(half * depth, (half + 1) * depth)
                 sum_out[row, :, columns] = after[piece]
                 theta_out[row, :, columns] = later[piece]
             return carry
@@ -489,9 +515,9 @@
             VMEM((lines, cells), single),
             VMEM((lines, cells), single),
             VMEM((lines + 2 * HALO * depth, cells + 2 * LANES), single),
-            VMEM((lines, cells), single),
-            VMEM((lines, cells), single),
-            pltpu.SemaphoreType.DMA((7,)),
+            VMEM(theta.shape, single),
+            VMEM(theta.shape, single),
+            pltpu.SemaphoreType.DMA((9,)),
             pltpu.SemaphoreType.DMA((2, 3, gz)),
             pltpu.SemaphoreType.DMA((2, 3, gx - 1)),
             pltpu.SemaphoreType.DMA((2, 4)),

time: 31.1 us -> 28.8 us (0.926)
  Pallas kernels: 30.3 us -> 28 us
    pallas_call x1, Pallas kernels: 29.5 us -> 27.2 us  [body(): pl.pallas_call(functools.partial(section_kernel, sizes, span), out_shape=...]
where the time goes in v4:
time: 28.8 us; the launch traced here: 28.6 us
  Pallas kernels  28 us (97%)
  between operations  0.64 us (2%)
    pallas_call x1, Pallas kernels, body(): pl.pallas_call(functools.partial(section_kernel, sizes, span), out_shape=...  27.2 us
    pallas_call x1, Pallas kernels, body(): pl.pallas_call(put, out_shape=[jax.ShapeDtypeStruct(theta.shape, single)]...  0.81 us

profile of v4, /device:TPU:0, one launch (start us, length us, event | category | flops | bytes accessed | tf_op | source)
XLA Modules:
  0.0 28.6 jit_solution(7580739349033173951)
XLA Ops:
  0.6 27.2 %section.1 = (f32[8,4,2048]{2,1,0:T(4,128)S(1)}, f32[8,4,2048]{2,1,0:T(4,128)S(1)}) custom-call(s32[4]{0:T(128)} %offset_ref.1, s32[4]{0:T(128)} %length_ref.1, f32[3,2,2,16,512]{4,3,2,1,0:T(8,128)} %spec_hbm.1, f32[8,4,2048]{2,1,0:T(4,128)} %theta_hbm.1, f32[8,4,2048]{2,1,0:T(4,128)} %sum_hbm.1, s32[8,8192]{1,0:T(8,128)} %index_hbm.1, ...), custom_call_target="tpu_custom_call" | custom-call | tf_op jit(solution)/shard_map/section/pallas_call | solution.py:491
  27.8 0.8 %put.1 = (f32[8,4,2048]{2,1,0:T(4,128)}, f32[8,4,2048]{2,1,0:T(4,128)}) custom-call(f32[8,4,2048]{2,1,0:T(4,128)S(1)} %get-tuple-element.4.theta_ref, f32[8,4,2048]{2,1,0:T(4,128)S(1)} %get-tuple-element.5.sum_ref), custom_call_target="tpu_custom_call" | custom-call | tf_op jit(solution)/shard_map/put/pallas_call | solution.py:535

commit v5 on v4

--- a/solution.py
+++ b/solution.py
@@ -70,7 +70,7 @@
     spec_ref, theta_ref, sum_ref, index_ref, weight_ref, twist_ref, last_ref,
     modes_send, modes_recv, mixed, velocity, seg_send, seg_recv, matrix_top, matrix_rest, gathered, values,
     grads, part, drift, field, z_back, z_front,
-    load_sems, modes_sems, seg_sems, face_sems, deep_sems,
+    load_sems, modes_sems, seg_sems, face_sems, deep_sems, meet_sems,
 ):
     gx, gy, gz = sizes
     here = {axis: lax.axis_index(axis) for axis in ("gx", "gy", "gz")}
@@ -118,13 +118,23 @@
     def signal(semaphore, target):
         pl.semaphore_signal(semaphore, inc=1, device_id=target, device_id_type=MESH)
 
-    targets = [{"gx": lax.rem(me + step, gx)} for step in range(1, gx)]
-    targets += [{"gz": lax.rem(layer + step, gz)} for step in range(1, gz)]
-    targets += [ahead["gy"], behind["gy"]]
-    for target in targets:
+    hub = layer == 0
+    column = [{"gz": lax.rem(layer + step, gz)} for step in range(1, gz)]
+    beside = [{"gx": lax.rem(me + step, gx)} for step in range(1, gx)] + [ahead["gy"], behind["gy"]]
+    for target in column:
         signal(barrier, target)
 
-    pl.semaphore_wait(barrier, len(targets))
+    @pl.when(hub)
+    def _():
+        for target in beside:
+            signal(barrier, target)
+        pl.semaphore_wait(barrier, len(column) + len(beside))
+        for target in beside:
+            signal(meet_sems.at[0], target)
+
+    @pl.when(jnp.logical_not(hub))
+    def _():
+        pl.semaphore_wait(barrier, len(column))
 
     def modes_copy(comp, target):
         return pltpu.make_async_remote_copy(
@@ -243,8 +253,6 @@
             ]
         )
     ]
-    for face in faces:
-        face.start()
 
     for comp in range(3):
         modes_recv[comp, layer] = modes_send[comp, layer]
@@ -297,8 +305,25 @@
         return lax.fori_loop(0, span, slab_of, carry)
 
     chunks = cells // LANES
-    early, step_of = chunks * 3 // 8, chunks // 8
-    lax.fori_loop(0, early, build, 0)
+    step_of = chunks // 8
+    early = chunks - 4 * step_of
+    first = chunks * 4 // 16
+    lax.fori_loop(0, first, build, 0)
+
+    @pl.when(hub)
+    def _():
+        pl.semaphore_wait(meet_sems.at[0], len(beside))
+        for target in column:
+            signal(meet_sems.at[1], target)
+
+    lax.fori_loop(first, early, build, 0)
+
+    @pl.when(jnp.logical_not(hub))
+    def _():
+        pl.semaphore_wait(meet_sems.at[1], 1)
+
+    for face in faces:
+        face.start()
 
     loads[6].wait()
     loads[7].wait()
@@ -522,6 +547,7 @@
             pltpu.SemaphoreType.DMA((2, 3, gx - 1)),
             pltpu.SemaphoreType.DMA((2, 4)),
             pltpu.SemaphoreType.DMA((2, 2, tiles)),
+            pltpu.SemaphoreType.REGULAR((2,)),
         ],
         compiler_params=pltpu.CompilerParams(
             collective_id=0, has_side_effects=True, vmem_limit_bytes=60 * 1024 * 1024

time: 28.8 us -> 28.1 us (0.976)
  Pallas kernels: 28 us -> 27.3 us
    pallas_call x1, Pallas kernels: 27.2 us -> 26.5 us  [body(): pl.pallas_call(functools.partial(section_kernel, sizes, span), out_shape=...]
where the time goes in v5:
time: 28.1 us; the launch traced here: 27.9 us
  Pallas kernels  27.3 us (97%)
  between operations  0.64 us (2%)
    pallas_call x1, Pallas kernels, body(): pl.pallas_call(functools.partial(section_kernel, sizes, span), out_shape=...  26.5 us
    pallas_call x1, Pallas kernels, body(): pl.pallas_call(put, out_shape=[jax.ShapeDtypeStruct(theta.shape, single)]...  0.81 us

profile of v5, /device:TPU:0, one launch (start us, length us, event | category | flops | bytes accessed | tf_op | source)
XLA Modules:
  0.0 27.9 jit_solution(14583856149283260494)
XLA Ops:
  0.6 26.5 %section.1 = (f32[8,4,2048]{2,1,0:T(4,128)S(1)}, f32[8,4,2048]{2,1,0:T(4,128)S(1)}) custom-call(s32[4]{0:T(128)} %offset_ref.1, s32[4]{0:T(128)} %length_ref.1, f32[3,2,2,16,512]{4,3,2,1,0:T(8,128)} %spec_hbm.1, f32[8,4,2048]{2,1,0:T(4,128)} %theta_hbm.1, f32[8,4,2048]{2,1,0:T(4,128)} %sum_hbm.1, s32[8,8192]{1,0:T(8,128)} %index_hbm.1, ...), custom_call_target="tpu_custom_call" | custom-call | tf_op jit(solution)/shard_map/section/pallas_call | solution.py:516
  27.1 0.8 %put.1 = (f32[8,4,2048]{2,1,0:T(4,128)}, f32[8,4,2048]{2,1,0:T(4,128)}) custom-call(f32[8,4,2048]{2,1,0:T(4,128)S(1)} %get-tuple-element.4.theta_ref, f32[8,4,2048]{2,1,0:T(4,128)S(1)} %get-tuple-element.5.sum_ref), custom_call_target="tpu_custom_call" | custom-call | tf_op jit(solution)/shard_map/put/pallas_call | solution.py:561

commit v6 on v5

--- a/solution.py
+++ b/solution.py
@@ -306,7 +306,7 @@
 
     chunks = cells // LANES
     step_of = chunks // 8
-    early = chunks - 4 * step_of
+    early = chunks - 5 * step_of
     first = chunks * 4 // 16
     lax.fori_loop(0, first, build, 0)
 

time: 28.1 us -> 27.5 us (0.979)
  Pallas kernels: 27.3 us -> 26.7 us
    pallas_call x1, Pallas kernels: 26.5 us -> 25.9 us  [body(): pl.pallas_call(functools.partial(section_kernel, sizes, span), out_shape=...]
where the time goes in v6:
time: 27.5 us; the launch traced here: 27.4 us
  Pallas kernels  26.7 us (97%)
  between operations  0.64 us (2%)
    pallas_call x1, Pallas kernels, body(): pl.pallas_call(functools.partial(section_kernel, sizes, span), out_shape=...  25.9 us
    pallas_call x1, Pallas kernels, body(): pl.pallas_call(put, out_shape=[jax.ShapeDtypeStruct(theta.shape, single)]...  0.81 us

profile of v6, /device:TPU:0, one launch (start us, length us, event | category | flops | bytes accessed | tf_op | source)
XLA Modules:
  0.0 27.4 jit_solution(2270312339949663955)
XLA Ops:
  0.6 25.9 %section.1 = (f32[8,4,2048]{2,1,0:T(4,128)S(1)}, f32[8,4,2048]{2,1,0:T(4,128)S(1)}) custom-call(s32[4]{0:T(128)} %offset_ref.1, s32[4]{0:T(128)} %length_ref.1, f32[3,2,2,16,512]{4,3,2,1,0:T(8,128)} %spec_hbm.1, f32[8,4,2048]{2,1,0:T(4,128)} %theta_hbm.1, f32[8,4,2048]{2,1,0:T(4,128)} %sum_hbm.1, s32[8,8192]{1,0:T(8,128)} %index_hbm.1, ...), custom_call_target="tpu_custom_call" | custom-call | tf_op jit(solution)/shard_map/section/pallas_call | solution.py:516
  26.5 0.8 %put.1 = (f32[8,4,2048]{2,1,0:T(4,128)}, f32[8,4,2048]{2,1,0:T(4,128)}) custom-call(f32[8,4,2048]{2,1,0:T(4,128)S(1)} %get-tuple-element.4.theta_ref, f32[8,4,2048]{2,1,0:T(4,128)S(1)} %get-tuple-element.5.sum_ref), custom_call_target="tpu_custom_call" | custom-call | tf_op jit(solution)/shard_map/put/pallas_call | solution.py:561

commit v7 on v6

--- a/solution.py
+++ b/solution.py
@@ -65,9 +65,9 @@
 
 def section_kernel(
     sizes, span,
-    offset_ref, length_ref, spec_hbm, theta_hbm, sum_hbm, index_hbm, weight_hbm, twist_hbm, last_hbm,
+    offset_hbm, length_hbm, spec_hbm, theta_hbm, sum_hbm, index_hbm, weight_hbm, twist_hbm, last_hbm,
     theta_out, sum_out,
-    spec_ref, theta_ref, sum_ref, index_ref, weight_ref, twist_ref, last_ref,
+    offset_ref, length_ref, spec_ref, theta_ref, sum_ref, index_ref, weight_ref, twist_ref, last_ref,
     modes_send, modes_recv, mixed, velocity, seg_send, seg_recv, matrix_top, matrix_rest, gathered, values,
     grads, part, drift, field, z_back, z_front,
     load_sems, modes_sems, seg_sems, face_sems, deep_sems, meet_sems,
@@ -90,6 +90,25 @@
     tiles = lines // TILE
     skirt = HALO * depth
 
+    barrier = pltpu.get_barrier_semaphore()
+    has_up, has_down = layer < gz - 1, layer > 0
+    inner = jnp.logical_and(has_up, has_down)
+    per_tile = TILE // depth
+
+    def signal(semaphore, target):
+        pl.semaphore_signal(semaphore, inc=1, device_id=target, device_id_type=MESH)
+
+    hub = layer == 0
+    column = [{"gz": lax.rem(layer + step, gz)} for step in range(1, gz)]
+    beside = [{"gx": lax.rem(me + step, gx)} for step in range(1, gx)] + [ahead["gy"], behind["gy"]]
+    for target in column:
+        signal(barrier, target)
+
+    @pl.when(hub)
+    def _():
+        for target in beside:
+            signal(barrier, target)
+
     own_columns = pl.ds(pl.multiple_of(me * cells, LANES), cells)
     loads = [
         pltpu.make_async_copy(source, place, load_sems.at[number])
@@ -104,30 +123,16 @@
                 (twist_hbm, twist_ref),
                 (last_hbm, last_ref),
                 (sum_hbm, sum_ref),
+                (offset_hbm, offset_ref),
+                (length_hbm, length_ref),
             ]
         )
     ]
     for load in loads:
         load.start()
 
-    barrier = pltpu.get_barrier_semaphore()
-    has_up, has_down = layer < gz - 1, layer > 0
-    inner = jnp.logical_and(has_up, has_down)
-    per_tile = TILE // depth
-
-    def signal(semaphore, target):
-        pl.semaphore_signal(semaphore, inc=1, device_id=target, device_id_type=MESH)
-
-    hub = layer == 0
-    column = [{"gz": lax.rem(layer + step, gz)} for step in range(1, gz)]
-    beside = [{"gx": lax.rem(me + step, gx)} for step in range(1, gx)] + [ahead["gy"], behind["gy"]]
-    for target in column:
-        signal(barrier, target)
-
     @pl.when(hub)
     def _():
-        for target in beside:
-            signal(barrier, target)
         pl.semaphore_wait(barrier, len(column) + len(beside))
         for target in beside:
             signal(meet_sems.at[0], target)
@@ -259,6 +264,8 @@
 
     loads[4].wait()
     loads[5].wait()
+    loads[9].wait()
+    loads[10].wait()
     live_count = length_ref[me]
     begin = offset_ref[me] - jnp.minimum(offset_ref[me] // LANES, far - span) * LANES
     counter = lax.broadcasted_iota(jnp.int32, (LANES, LANES), 0).astype(jnp.float32).astype(jnp.bfloat16)
@@ -516,9 +523,11 @@
     held = pl.pallas_call(
         functools.partial(section_kernel, sizes, span),
         out_shape=[VMEM(theta.shape, single)] * 2,
-        in_specs=[pl.BlockSpec(memory_space=pltpu.SMEM)] * 2 + [pl.BlockSpec(memory_space=pltpu.HBM)] * 7,
+        in_specs=[pl.BlockSpec(memory_space=pltpu.HBM)] * 9,
         out_specs=whole_vmem(2),
         scratch_shapes=[
+            pltpu.SMEM(seg_offset.shape, jnp.int32),
+            pltpu.SMEM(seg_length.shape, jnp.int32),
             VMEM(spectrum.shape, single),
             VMEM(theta.shape, single),
             VMEM(theta.shape, single),
@@ -542,7 +551,7 @@
             VMEM((lines + 2 * HALO * depth, cells + 2 * LANES), single),
             VMEM(theta.shape, single),
             VMEM(theta.shape, single),
-            pltpu.SemaphoreType.DMA((9,)),
+            pltpu.SemaphoreType.DMA((11,)),
             pltpu.SemaphoreType.DMA((2, 3, gz)),
             pltpu.SemaphoreType.DMA((2, 3, gx - 1)),
             pltpu.SemaphoreType.DMA((2, 4)),

time: 27.5 us -> 26.9 us (0.978)
  Pallas kernels: 26.7 us -> 26.1 us
    pallas_call x1, Pallas kernels: 25.9 us -> 25.3 us  [body(): pl.pallas_call(functools.partial(section_kernel, sizes, span), out_shape=...]
where the time goes in v7:
time: 26.9 us; the launch traced here: 26.7 us
  Pallas kernels  26.1 us (97%)
  between operations  0.64 us (2%)
    pallas_call x1, Pallas kernels, body(): pl.pallas_call(functools.partial(section_kernel, sizes, span), out_shape=...  25.3 us
    pallas_call x1, Pallas kernels, body(): pl.pallas_call(put, out_shape=[jax.ShapeDtypeStruct(theta.shape, single)]...  0.81 us

profile of v7, /device:TPU:0, one launch (start us, length us, event | category | flops | bytes accessed | tf_op | source)
XLA Modules:
  0.0 26.7 jit_solution(7736750103050180950)
XLA Ops:
  0.6 25.3 %section.1 = (f32[8,4,2048]{2,1,0:T(4,128)S(1)}, f32[8,4,2048]{2,1,0:T(4,128)S(1)}) custom-call(s32[4]{0:T(128)} %offset_hbm.1, s32[4]{0:T(128)} %length_hbm.1, f32[3,2,2,16,512]{4,3,2,1,0:T(8,128)} %spec_hbm.1, f32[8,4,2048]{2,1,0:T(4,128)} %theta_hbm.1, f32[8,4,2048]{2,1,0:T(4,128)} %sum_hbm.1, s32[8,8192]{1,0:T(8,128)} %index_hbm.1, ...), custom_call_target="tpu_custom_call" | custom-call | tf_op jit(solution)/shard_map/section/pallas_call | solution.py:523
  25.9 0.8 %put.1 = (f32[8,4,2048]{2,1,0:T(4,128)}, f32[8,4,2048]{2,1,0:T(4,128)}) custom-call(f32[8,4,2048]{2,1,0:T(4,128)S(1)} %get-tuple-element.4.theta_ref, f32[8,4,2048]{2,1,0:T(4,128)S(1)} %get-tuple-element.5.sum_ref), custom_call_target="tpu_custom_call" | custom-call | tf_op jit(solution)/shard_map/put/pallas_call | solution.py:570

commit v8 on v7

--- a/solution.py
+++ b/solution.py
@@ -131,6 +131,18 @@
     for load in loads:
         load.start()
 
+    def repack(comp):
+        loads[comp].wait()
+        for slab in range(local_slabs):
+            for part_of in range(2):
+                for row in range(own_rows):
+                    held = spec_ref[comp, part_of, row, :, slab * LANES : (slab + 1) * LANES]
+                    at = part_of * group + row * depth
+                    for peer in range(gz):
+                        modes_send[comp, peer, slab, at : at + depth, :] = held[
+                            peer * depth : (peer + 1) * depth
+                        ]
+
     @pl.when(hub)
     def _():
         pl.semaphore_wait(barrier, len(column) + len(beside))
@@ -187,25 +199,27 @@
             for tile in chosen:
                 deep_copy(0, tile).start()
 
-        @pl.when(has_down)
+        @pl.when(jnp.logical_and(has_down, has_up))
         def _():
             for tile in chosen:
                 deep_copy(1, tile).start()
 
+        @pl.when(jnp.logical_not(has_up))
+        def _():
+            for tile in chosen:
+                if tile > 0:
+                    deep_copy(1, tile).start()
+
+    @pl.when(layer == gz - 1)
+    def _():
+        deep_copy(1, 0).start()
+
     for comp in range(3):
-        loads[comp].wait()
-        for slab in range(local_slabs):
-            for part_of in range(2):
-                for row in range(own_rows):
-                    held = spec_ref[comp, part_of, row, :, slab * LANES : (slab + 1) * LANES]
-                    at = part_of * group + row * depth
-                    for peer in range(gz):
-                        modes_send[comp, peer, slab, at : at + depth, :] = held[
-                            peer * depth : (peer + 1) * depth
-                        ]
+        if comp >= 0:
+            repack(comp)
         for distance in range(gz - 1, 0, -1):
             send_modes(comp, distance)
-    send_near(range(tiles))
+    send_near(range(tiles - 1))
 
     @pl.when(jnp.logical_not(inner))
     def _():
@@ -218,6 +232,8 @@
         def _():
             for tile in range(tiles):
                 deep_copy(1, tile).start()
+
+    send_near(range(tiles - 1, tiles))
 
     def seg_copy(comp, step):
         target = lax.rem(me + step, gx)

time: 26.9 us -> 26.7 us (level)
  no operation moved by 1% of the time
where the time goes in v8:
time: 26.7 us; the launch traced here: 26.5 us
  Pallas kernels  25.9 us (97%)
  between operations  0.64 us (2%)
    pallas_call x1, Pallas kernels, body(): pl.pallas_call(functools.partial(section_kernel, sizes, span), out_shape=...  25.1 us
    pallas_call x1, Pallas kernels, body(): pl.pallas_call(put, out_shape=[jax.ShapeDtypeStruct(theta.shape, single)]...  0.81 us

profile of v8, /device:TPU:0, one launch (start us, length us, event | category | flops | bytes accessed | tf_op | source)
XLA Modules:
  0.0 26.5 jit_solution(9492010357989792621)
XLA Ops:
  0.6 25.1 %section.1 = (f32[8,4,2048]{2,1,0:T(4,128)S(1)}, f32[8,4,2048]{2,1,0:T(4,128)S(1)}) custom-call(s32[4]{0:T(128)} %offset_hbm.1, s32[4]{0:T(128)} %length_hbm.1, f32[3,2,2,16,512]{4,3,2,1,0:T(8,128)} %spec_hbm.1, f32[8,4,2048]{2,1,0:T(4,128)} %theta_hbm.1, f32[8,4,2048]{2,1,0:T(4,128)} %sum_hbm.1, s32[8,8192]{1,0:T(8,128)} %index_hbm.1, ...), custom_call_target="tpu_custom_call" | custom-call | tf_op jit(solution)/shard_map/section/pallas_call | solution.py:539
  25.7 0.8 %put.1 = (f32[8,4,2048]{2,1,0:T(4,128)}, f32[8,4,2048]{2,1,0:T(4,128)}) custom-call(f32[8,4,2048]{2,1,0:T(4,128)S(1)} %get-tuple-element.4.theta_ref, f32[8,4,2048]{2,1,0:T(4,128)S(1)} %get-tuple-element.5.sum_ref), custom_call_target="tpu_custom_call" | custom-call | tf_op jit(solution)/shard_map/put/pallas_call | solution.py:586

commit v9 on v8

--- a/solution.py
+++ b/solution.py
@@ -14,7 +14,7 @@
 LANES = 128
 HALO = 4
 TILE = 8
-WIDTH = 512
+WIDTH = 1024
 
 first_coeffs = (0.8, -0.2, 4.0 / 105.0, -1.0 / 280.0)
 second_coeffs = (1.6, -0.2, 8.0 / 315.0, -1.0 / 560.0)

time: 26.7 us -> 26.6 us (level)
  no operation moved by 1% of the time
where the time goes in v9:
time: 26.6 us; the launch traced here: 26.4 us
  Pallas kernels  25.8 us (97%)
  between operations  0.64 us (2%)
    pallas_call x1, Pallas kernels, body(): pl.pallas_call(functools.partial(section_kernel, sizes, span), out_shape=...  25 us
    pallas_call x1, Pallas kernels, body(): pl.pallas_call(put, out_shape=[jax.ShapeDtypeStruct(theta.shape, single)]...  0.81 us

profile of v9, /device:TPU:0, one launch (start us, length us, event | category | flops | bytes accessed | tf_op | source)
XLA Modules:
  0.0 26.4 jit_solution(12460970996110565068)
XLA Ops:
  0.6 25.0 %section.1 = (f32[8,4,2048]{2,1,0:T(4,128)S(1)}, f32[8,4,2048]{2,1,0:T(4,128)S(1)}) custom-call(s32[4]{0:T(128)} %offset_hbm.1, s32[4]{0:T(128)} %length_hbm.1, f32[3,2,2,16,512]{4,3,2,1,0:T(8,128)} %spec_hbm.1, f32[8,4,2048]{2,1,0:T(4,128)} %theta_hbm.1, f32[8,4,2048]{2,1,0:T(4,128)} %sum_hbm.1, s32[8,8192]{1,0:T(8,128)} %index_hbm.1, ...), custom_call_target="tpu_custom_call" | custom-call | tf_op jit(solution)/shard_map/section/pallas_call | solution.py:539
  25.6 0.8 %put.1 = (f32[8,4,2048]{2,1,0:T(4,128)}, f32[8,4,2048]{2,1,0:T(4,128)}) custom-call(f32[8,4,2048]{2,1,0:T(4,128)S(1)} %get-tuple-element.4.theta_ref, f32[8,4,2048]{2,1,0:T(4,128)S(1)} %get-tuple-element.5.sum_ref), custom_call_target="tpu_custom_call" | custom-call | tf_op jit(solution)/shard_map/put/pallas_call | solution.py:586
